TPU v7x, 256 devices: a whole 4x4x8 slice. The times are simulated.
256 devices in a mesh: tp: 4 (over x), rep: 64 (over y, z, core).
Axes of the slice: x: 4, y: 4, z: 8, core: 2. Of those that a mesh axis runs over, the one named last changes fastest.
Arguments:
- queries: bfloat16 [1024, 4096], P('rep', 'tp'), may hold values from -6 to 6
- new_keys: bfloat16 [1024, 2048], P('rep', 'tp'), may hold values from -6 to 6
- new_values: bfloat16 [1024, 2048], P('rep', 'tp'), may hold values from -6 to 6
- stored_keys: bfloat16 [1024, 16, 128, 128], P('rep', 'tp'), may hold values from -6 to 6
- stored_values: bfloat16 [1024, 16, 128, 128], P('rep', 'tp'), may hold values from -6 to 6
- lengths: int32 [1024], P('rep'), may hold values from 1 to 128
- out_proj: bfloat16 [4096, 4608], P('tp', 'rep'), may hold values from -0.09375 to 0.09375
- residual: bfloat16 [1024, 4608], P(None, 'rep'), may hold values from -4.5 to 4.5
- norm_gain: float32 [4608], replicated, may hold values from 0.1 to 1.9
- embedding: bfloat16 [256000, 4608], P(('tp', 'rep')), may hold values from -1.25 to 1.25
- targets: int32 [1024], replicated, may hold values from 0 to 255999
- old_sums: float32 [1024], P('rep'), may hold values from -3 to 0
- rewards: float32 [1024], P('rep'), may hold values from -6 to 6
- group_ids: int32 [1024], P('rep'), may hold values from 0 to 127, as said below
Outputs:
- logprob_sum: float32 [1024], P('rep')
- advantage: float32 [1024], P('rep')
Inputs may be any that keep to these rules, and one draw needn't show every extreme that they name: `group_ids`: each id names exactly 8 continuations.
All inputs are finite; a program needn't handle non-finite values.
Results may differ from a plain program's by a relative error of at most 0.001.
Values may be sent and summed in bfloat16 or wider, within the bound.
No kernel may reach another device: no remote copies, remote signals or barrier semaphores. Data moves between devices by JAX's collectives and lax.ppermute only.
A program may use at most 64 MiB of HBM per device.

v0:
```python
import jax
import jax.numpy as jnp
from jax import lax
from jax.sharding import Mesh
from jax.sharding import PartitionSpec as P

D = 4608
GROUP = 8
REP = ("rep_0", "rep_1", "rep_2")
TP_REP = ("tp", "rep_0", "rep_1", "rep_2")


def sent_to_all(x, axis):
    devices = lax.axis_size(axis)
    return lax.all_to_all(jnp.broadcast_to(x[None], (devices, *x.shape)), axis, 0, 0, tiled=True)


def of_everyone(x, axis):
    everything = sent_to_all(x, axis)
    return jnp.sum(everything, axis=0)


def laid_out(blocks, dim):
    lengths = list(blocks.shape[1:])
    lengths[dim] *= blocks.shape[0]
    return jnp.moveaxis(blocks, 0, dim).reshape(lengths)


def whole_of(x, axes, dim):
    far, near = axes
    blocks = sent_to_all(sent_to_all(x, far), near)
    return laid_out(blocks.swapaxes(0, 1).reshape(-1, *x.shape), dim)


def over_axes(x, axes):
    far, near = axes
    nearer = of_everyone(x, near)
    return of_everyone(nearer, far)


def packed_total(arrays, axis):
    ravelled, at, finished = (jnp.concatenate([a.reshape(-1) for a in arrays]), 0, [])
    subtotal = over_axes(ravelled, axis)
    for a in arrays:
        finished.append(subtotal[at : at + a.size].reshape(a.shape))
        at += a.size
    return tuple(finished)


def attention(queries, new_keys, new_values, stored_keys, stored_values, lengths):
    samp, heads_kv, span, depth = stored_keys.shape
    sample_ratio = queries.shape[1] // (heads_kv * depth)
    query_vector = queries.reshape(samp, heads_kv, sample_ratio, depth)
    scores = (
        jnp.einsum("sgqd,sgpd->sgqp", query_vector, stored_keys, preferred_element_type=jnp.float32)
        / 12.0
    )
    scores = 50.0 * jnp.tanh(scores / 50.0)
    valid = lax.broadcasted_iota(jnp.int32, (samp, 1, 1, span), 3) < lengths[:, None, None, None]
    expo = jnp.where(valid, jnp.exp(scores), 0.0)
    own_logit = (
        jnp.einsum(
            "sgqd,sgd->sgq",
            query_vector,
            new_keys.reshape(samp, heads_kv, depth),
            preferred_element_type=jnp.float32,
        )
        / 12.0
    )
    own_logit = 50.0 * jnp.tanh(own_logit / 50.0)
    own_exp = jnp.exp(own_logit)
    total = jnp.sum(expo, -1) + own_exp
    probs = (expo / total[..., None]).astype(jnp.bfloat16)
    own_probability = (own_exp / total).astype(jnp.bfloat16)
    attended_output = jnp.einsum(
        "sgqp,sgpd->sgqd", probs, stored_values, preferred_element_type=jnp.float32
    )
    attended_output = attended_output + own_probability.astype(jnp.float32)[
        ..., None
    ] * new_values.reshape(samp, heads_kv, 1, depth).astype(jnp.float32)
    return attended_output.reshape(samp, sample_ratio * heads_kv * depth).astype(jnp.bfloat16)


def per_device(
    queries,
    new_keys,
    new_values,
    stored_keys,
    stored_values,
    lengths,
    out_proj,
    residual,
    norm_gain,
    embedding,
    targets,
    old_sums,
    rewards,
    group_ids,
):
    samp = queries.shape[0]
    reps = lax.axis_size(REP)
    rep_index = lax.axis_index(REP)
    tp_index = lax.axis_index("tp")
    groups = samp * reps // GROUP
    member = group_ids[:, None] == lax.broadcasted_iota(jnp.int32, (1, groups), 1)
    reward_part = jnp.sum(jnp.where(member, rewards[:, None], 0.0), 0)
    group_total = of_everyone(reward_part, REP)
    mine = jnp.sum(jnp.where(member, group_total[None, :], 0.0), 1)
    advantage = rewards - (mine - rewards) / (GROUP - 1.0)
    context = attention(queries, new_keys, new_values, stored_keys, stored_values, lengths)
    partial_value = jnp.dot(
        whole_of(context, (("rep_0", "rep_1"), "rep_2"), 0),
        out_proj,
        preferred_element_type=jnp.float32,
    )
    columns = residual.shape[1]
    vocab_rows = embedding.shape[0]
    contract = (((1,), (1,)), ((), ()))
    heads = of_everyone(partial_value, "tp")
    stream = residual.astype(jnp.float32) + heads
    squares = of_everyone(jnp.sum(stream * stream, 1), REP)
    scale = lax.rsqrt(squares / D + 1e-06)
    gain_part = lax.dynamic_slice_in_dim(norm_gain, rep_index * columns, columns)
    normed = (stream * scale[:, None] * gain_part[None, :]).astype(jnp.bfloat16)
    gathered = lax.all_gather(normed, REP, axis=1, tiled=True)
    logits = lax.dot_general(gathered, embedding, contract, preferred_element_type=jnp.float32)
    capped = 30.0 * jnp.tanh(logits / 30.0)
    offset = (tp_index * reps + rep_index) * vocab_rows
    entry_ids = offset + lax.broadcasted_iota(jnp.int32, (1, vocab_rows), 1)
    picked_part = jnp.sum(jnp.where(entry_ids == targets[:, None], capped, 0.0), 1)
    total, picked = packed_total(
        (jnp.sum(jnp.exp(capped), 1), picked_part), (("tp", "rep_0"), ("rep_1", "rep_2"))
    )
    logprob = picked - jnp.log(total)
    own_rows = lax.dynamic_slice_in_dim(logprob, rep_index * samp, samp)
    logprob_sum = old_sums + own_rows
    return (logprob_sum, advantage)


def solution(mesh):
    split = Mesh(mesh.devices.reshape(mesh.shape["tp"], 4, 8, 2), ("tp", "rep_0", "rep_1", "rep_2"))
    placed = (
        P(REP, "tp"),
        P(REP, "tp"),
        P(REP, "tp"),
        P(REP, "tp", None, None),
        P(REP, "tp", None, None),
        P(REP),
        P("tp", REP),
        P(None, REP),
        P(),
        P(TP_REP, None),
        P(),
        P(REP),
        P(REP),
        P(REP),
    )
    return jax.shard_map(
        per_device, mesh=split, in_specs=placed, out_specs=(P(REP), P(REP)), check_vma=False
    )
```

profile of v0, /device:TPU:1, one launch (start us, length us, event | category | flops | bytes accessed | tf_op | source)
XLA Modules:
  0.0 235.7 jit_solution(11303239664290411377)
XLA Ops:
  7.2 0.9 reshape.88
  8.1 0.7 iota_compare_fusion.1
  8.8 1.3 fusion.12
  10.2 0.7 reshape.94
  11.5 0.7 reshape.90
  12.3 2.3 fusion.4
  14.7 36.7 %all_to_all.39 = bf16[32,16,1024]{2,1,0:T(8,128)(2,1)S(1)} all-to-all(bf16[32,16,1024]{2,1,0:T(8,128)(2,1)S(1)} %broadcast_in_dim.53), channel_id=1, replica_groups=mesh['tp'=4,'rep_0'=4,'rep_1'=8,'rep_2'=2] {'rep_0','rep_1'}, dimensions={0} | all-to-all | bytes 2097152 | tf_op jit(solution)/shard_map/all_to_all | solution.py:15
  51.7 9.9 %all_to_all.40 = bf16[2,32,16,1024]{3,2,1,0:T(8,128)(2,1)S(1)} all-to-all(bf16[2,32,16,1024]{3,2,1,0:T(8,128)(2,1)S(1)} %broadcast_in_dim.55), channel_id=1, replica_groups=mesh['tp'=4,'rep_0'=4,'rep_1'=8,'rep_2'=2] {'rep_2'}, dimensions={0} | all-to-all | bytes 4194304 | tf_op jit(solution)/shard_map/all_to_all | solution.py:15
  61.9 0.8 fusion.14
  62.9 19.5 %all_to_all.41 = f32[4,1024,72]{1,2,0:T(8,128)S(1)} all-to-all(f32[4,1024,72]{1,2,0:T(8,128)S(1)} %broadcast_in_dim.56), channel_id=1, replica_groups=mesh['tp'=4,'rep_0'=4,'rep_1'=8,'rep_2'=2] {'tp'}, dimensions={0} | all-to-all | bytes 2359296 | tf_op jit(solution)/shard_map/all_to_all | solution.py:15
  82.3 0.8 reduce_sum.100
  83.1 1.0 multiply_reduce_fusion
  84.2 0.8 broadcast_in_dim.57
  85.0 7.1 %all-to-all-start.3 = ((f32[64,1,1024]{2,1,0:T(1,128)}), f32[64,1,1024]{2,1,0:T(1,128)S(1)}, u32[]{:S(2)}, u32[]{:S(2)}) async-start(f32[64,1,1024]{2,1,0:T(1,128)} %broadcast_in_dim.57), calls=%async_computation.3 | async-start | bytes 524288 | tf_op jit(solution)/shard_map/all_to_all | solution.py:15
  92.1 0.8 dynamic_slice.6
  92.9 11.1 %all-to-all-done.3 = f32[64,1,1024]{2,1,0:T(1,128)S(1)} async-done(((f32[64,1,1024]{2,1,0:T(1,128)}), f32[64,1,1024]{2,1,0:T(1,128)S(1)}, u32[]{:S(2)}, u32[]{:S(2)}) %all-to-all-start.3) | async-done | bytes 262176 | tf_op jit(solution)/shard_map/all_to_all | solution.py:15
  104.2 1.7 multiply_convert_fusion
  106.7 6.0 %all-to-all-start.6 = ((f32[64,1,128]{2,1,0:T(1,128)}), f32[64,1,128]{2,1,0:T(1,128)S(1)}, u32[]{:S(2)}, u32[]{:S(2)}) async-start(f32[64,1,128]{2,1,0:T(1,128)} %broadcast_in_dim.100), calls=%async_computation.6 | async-start | bytes 65536 | tf_op jit(solution)/shard_map/all_to_all | solution.py:15
  112.8 72.8 %all-gather.2.cloned.1.call-done = bf16[1024,4608]{0,1:T(8,128)(2,1)} async-done(((bf16[1024,72]{0,1:T(8,128)(2,1)}), bf16[1024,4608]{0,1:T(8,128)(2,1)}) %all-gather.2.cloned.1.call-update) | async-done | bytes 9437200 | tf_op jit(solution)/shard_map/all_gather | solution.py:125
  185.6 15.7 %exponential_reduce_fusion = (f32[1024]{0:T(1024)S(1)}, f32[1024]{0:T(1024)S(1)}) fusion(s32[1024]{0:T(1024)S(1)} %copy-done.4, s32[1000]{0:T(1024)S(1)} %iota_add_fusion, bf16[1024,4608]{0,1:T(8,128)(2,1)} %all-gather.2.cloned.1.call-done, bf16[1000,4608]{1,0:T(8,128)(2,1)} %param.23), kind=kOutput, calls=%fused_computation.1 | convolution fusion | flops 9443325952 | bytes 18669472 | tf_op jit(solution)/shard_map/dot_general | solution.py:126
  202.1 4.7 %all-to-all-start.4 = ((f32[16,1,2048]{2,1,0:T(1,128)}), f32[16,1,2048]{2,1,0:T(1,128)S(1)}, u32[]{:S(2)}, u32[]{:S(2)}) async-start(f32[16,1,2048]{2,1,0:T(1,128)} %broadcast_in_dim.59), calls=%async_computation.4 | async-start | bytes 262144 | tf_op jit(solution)/shard_map/all_to_all | solution.py:15
  206.9 8.7 %all-to-all-done.4 = f32[16,1,2048]{2,1,0:T(1,128)S(1)} async-done(((f32[16,1,2048]{2,1,0:T(1,128)}), f32[16,1,2048]{2,1,0:T(1,128)S(1)}, u32[]{:S(2)}, u32[]{:S(2)}) %all-to-all-start.4) | async-done | bytes 131104 | tf_op jit(solution)/shard_map/all_to_all | solution.py:15
  216.4 5.0 %all-to-all-start.5 = ((f32[16,1,2048]{2,1,0:T(1,128)}), f32[16,1,2048]{2,1,0:T(1,128)S(1)}, u32[]{:S(2)}, u32[]{:S(2)}) async-start(f32[16,1,2048]{2,1,0:T(1,128)} %broadcast_in_dim.60), calls=%async_computation.5 | async-start | bytes 262144 | tf_op jit(solution)/shard_map/all_to_all | solution.py:15
  221.9 6.3 %all-to-all-done.5 = f32[16,1,2048]{2,1,0:T(1,128)S(1)} async-done(((f32[16,1,2048]{2,1,0:T(1,128)}), f32[16,1,2048]{2,1,0:T(1,128)S(1)}, u32[]{:S(2)}, u32[]{:S(2)}) %all-to-all-start.5) | async-done | bytes 131104 | tf_op jit(solution)/shard_map/all_to_all | solution.py:15
  (43 shorter events, 5.4 us)
Async XLA Ops:
  7.2 1.7 copy-start
  51.7 10.2 %copy-start.2 = (bf16[1024,72]{0,1:T(8,128)(2,1)S(1)}, bf16[1024,72]{0,1:T(8,128)(2,1)}, u32[]{:S(2)}) copy-start(bf16[1024,72]{0,1:T(8,128)(2,1)} %param.20) | copy-start | bytes 442372
  61.9 21.2 %copy-start.1 = (bf16[1024,72]{0,1:T(8,128)(2,1)S(1)}, bf16[1024,72]{0,1:T(8,128)(2,1)}, u32[]{:S(2)}) copy-start(bf16[1024,72]{0,1:T(8,128)(2,1)} %param.21) | copy-start | bytes 442372
  62.7 43.2 %copy-start.5 = (s32[16]{0:T(128)S(1)}, s32[16]{0:T(128)}, u32[]{:S(2)}) copy-start(s32[16]{0:T(128)} %param.27) | copy-start | bytes 196
  62.7 43.2 %copy-start.6 = (f32[16]{0:T(128)S(1)}, f32[16]{0:T(128)}, u32[]{:S(2)}) copy-start(f32[16]{0:T(128)} %param.26) | copy-start | bytes 196
  62.7 122.9 %copy-start.4 = (s32[1024]{0:T(1024)S(1)}, s32[1024]{0:T(1024)}, u32[]{:S(2)}) copy-start(s32[1024]{0:T(1024)} %param.24) | copy-start | bytes 12292
  85.0 19.0 %all-to-all-start.3 = ((f32[64,1,1024]{2,1,0:T(1,128)}), f32[64,1,1024]{2,1,0:T(1,128)S(1)}, u32[]{:S(2)}, u32[]{:S(2)}) async-start(f32[64,1,1024]{2,1,0:T(1,128)} %broadcast_in_dim.57), calls=%async_computation.3 | async-start | bytes 524288 | tf_op jit(solution)/shard_map/all_to_all | solution.py:15
  92.0 93.6 %all-gather.2.cloned.1.call-start = ((), (), s32[]{:S(2)}) async-start(), calls=%async_computation.7 | async-start | bytes 9584640 | tf_op jit(solution)/shard_map/all_gather | solution.py:125
  106.7 94.7 %all-to-all-start.6 = ((f32[64,1,128]{2,1,0:T(1,128)}), f32[64,1,128]{2,1,0:T(1,128)S(1)}, u32[]{:S(2)}, u32[]{:S(2)}) async-start(f32[64,1,128]{2,1,0:T(1,128)} %broadcast_in_dim.100), calls=%async_computation.6 | async-start | bytes 65536 | tf_op jit(solution)/shard_map/all_to_all | solution.py:15
  112.7 115.5 %copy-start.3 = (f32[16]{0:T(128)S(1)}, f32[16]{0:T(128)}, u32[]{:S(2)}) copy-start(f32[16]{0:T(128)} %param.25) | copy-start | bytes 196
  202.1 13.5 %all-to-all-start.4 = ((f32[16,1,2048]{2,1,0:T(1,128)}), f32[16,1,2048]{2,1,0:T(1,128)S(1)}, u32[]{:S(2)}, u32[]{:S(2)}) async-start(f32[16,1,2048]{2,1,0:T(1,128)} %broadcast_in_dim.59), calls=%async_computation.4 | async-start | bytes 262144 | tf_op jit(solution)/shard_map/all_to_all | solution.py:15
  216.4 11.7 %all-to-all-start.5 = ((f32[16,1,2048]{2,1,0:T(1,128)}), f32[16,1,2048]{2,1,0:T(1,128)S(1)}, u32[]{:S(2)}, u32[]{:S(2)}) async-start(f32[16,1,2048]{2,1,0:T(1,128)} %broadcast_in_dim.60), calls=%async_computation.5 | async-start | bytes 262144 | tf_op jit(solution)/shard_map/all_to_all | solution.py:15
Sparse Core Ops, SparseCore 0:
  106.1 79.4 all-gather.1
where the time goes:
time: 237 us; the launch traced here: 236 us
  waiting for transfers between devices  98.9 us (42%)
  blocking collectives  66 us (28%)
  starting transfers between devices  22.8 us (10%)
  matrix products  20.3 us (9%)
  between operations  14.3 us (6%)
  local copies, waits for them, and re-layouts  7.36 us (3%)
  other arithmetic  6.06 us (3%)
    all_gather x1, waiting for transfers between devices, per_device(): gathered = lax.all_gather(normed, REP, axis=1, tiled=True)  72.8 us
    all_to_all x3, blocking collectives, sent_to_all(): lax.all_to_all(jnp.broadcast_to(x[None], (devices, *x.shape)), axis, 0, 0...  66 us
    all_to_all x4, waiting for transfers between devices, sent_to_all(): lax.all_to_all(jnp.broadcast_to(x[None], (devices, *x.shape)), axis, 0, 0...  26.1 us
    all_to_all x4, starting transfers between devices, sent_to_all(): lax.all_to_all(jnp.broadcast_to(x[None], (devices, *x.shape)), axis, 0, 0...  22.7 us
    dot_general x1, matrix products, per_device(): lax.dot_general(gathered, embedding, contract, preferred_element_type=jnp...  15.7 us
  transfers between devices with their start and end apart: 5, of which 4 were waited for; matrix products, arithmetic and copies ran while one was open for 8% of the time, Pallas kernels for 0%

commit v1 on v0

--- a/solution.py
+++ b/solution.py
@@ -3,11 +3,21 @@
 from jax import lax
 from jax.sharding import Mesh
 from jax.sharding import PartitionSpec as P
+from jax.lax import all_to_all, axis_size
 
 D = 4608
 GROUP = 8
 REP = ("rep_0", "rep_1", "rep_2")
 TP_REP = ("tp", "rep_0", "rep_1", "rep_2")
+
+
+def area_store(slab_in):
+    frames = []
+    for _ in range(axis_size(REP)):
+        frames.append(slab_in)
+    return jnp.concatenate(
+        all_to_all(jnp.stack(frames, axis=0), REP, split_axis=0, concat_axis=0), axis=1
+    )
 
 
 def sent_to_all(x, axis):
@@ -122,7 +132,7 @@
     scale = lax.rsqrt(squares / D + 1e-06)
     gain_part = lax.dynamic_slice_in_dim(norm_gain, rep_index * columns, columns)
     normed = (stream * scale[:, None] * gain_part[None, :]).astype(jnp.bfloat16)
-    gathered = lax.all_gather(normed, REP, axis=1, tiled=True)
+    gathered = area_store(normed)
     logits = lax.dot_general(gathered, embedding, contract, preferred_element_type=jnp.float32)
     capped = 30.0 * jnp.tanh(logits / 30.0)
     offset = (tp_index * reps + rep_index) * vocab_rows

time: 237 us -> 371 us (1.57)
  waiting for transfers between devices: 98.9 us -> 234 us
  between operations: 14.3 us -> 0.87 us
  starting transfers between devices: 22.8 us -> 31.3 us
  local copies, waits for them, and re-layouts: 7.36 us -> 12.2 us
    all_to_all x0 -> x1, waiting for transfers between devices: none -> 208 us  [area_store(): all_to_all(jnp.stack(frames, axis=0), REP, split_axis=0, concat_axis=0)]
    all_gather x1 -> x0, waiting for transfers between devices: 72.8 us -> none  [per_device(): gathered = lax.all_gather(normed, REP, axis=1, tiled=True)]
    all_to_all x0 -> x1, starting transfers between devices: none -> 6.33 us  [area_store(): all_to_all(jnp.stack(frames, axis=0), REP, split_axis=0, concat_axis=0)]
    another operation x0 -> x1, local copies, waits for them, and re-layouts: none -> 4.86 us  [area_store(): jnp.stack(frames, axis=0)]
  transfers between devices with their start and end apart: 5 -> 5, of which waited for: 4 -> 4; matrix products, arithmetic and copies ran while one was open for 8% -> 5% of each run, Pallas kernels for 0% -> 0%
where the time goes in v1:
time: 371 us; the launch traced here: 370 us
  waiting for transfers between devices  234 us (63%)
  blocking collectives  66 us (18%)
  starting transfers between devices  31.3 us (8%)
  matrix products  20.3 us (5%)
  local copies, waits for them, and re-layouts  12.2 us (3%)
  other arithmetic  5.4 us (1%)
    all_to_all x1, waiting for transfers between devices, area_store(): all_to_all(jnp.stack(frames, axis=0), REP, split_axis=0, concat_axis=0)  208 us
    all_to_all x3, blocking collectives, sent_to_all(): lax.all_to_all(jnp.broadcast_to(x[None], (devices, *x.shape)), axis, 0, 0...  66 us
    all_to_all x4, waiting for transfers between devices, sent_to_all(): lax.all_to_all(jnp.broadcast_to(x[None], (devices, *x.shape)), axis, 0, 0...  26.1 us
    all_to_all x4, starting transfers between devices, sent_to_all(): lax.all_to_all(jnp.broadcast_to(x[None], (devices, *x.shape)), axis, 0, 0...  24.9 us
    dot_general x1, matrix products, per_device(): lax.dot_general(gathered, embedding, contract, preferred_element_type=jnp...  15.7 us
  transfers between devices with their start and end apart: 5, of which 4 were waited for; matrix products, arithmetic and copies ran while one was open for 5% of the time, Pallas kernels for 0%

profile of v1, /device:TPU:1, one launch (start us, length us, event | category | flops | bytes accessed | tf_op | source)
XLA Modules:
  0.0 370.3 jit_solution(1938913209168502390)
XLA Ops:
  0.6 0.9 reshape.96
  2.3 1.3 fusion.12
  3.7 0.7 reshape.104
  5.7 2.3 fusion.4
  8.2 36.7 %all_to_all.44 = bf16[32,16,1024]{2,1,0:T(8,128)(2,1)S(1)} all-to-all(bf16[32,16,1024]{2,1,0:T(8,128)(2,1)S(1)} %broadcast_in_dim.53), channel_id=1, replica_groups=mesh['tp'=4,'rep_0'=4,'rep_1'=8,'rep_2'=2] {'rep_0','rep_1'}, dimensions={0} | all-to-all | bytes 2097152 | tf_op jit(solution)/shard_map/all_to_all | solution.py:25
  45.2 9.9 %all_to_all.45 = bf16[2,32,16,1024]{3,2,1,0:T(8,128)(2,1)S(1)} all-to-all(bf16[2,32,16,1024]{3,2,1,0:T(8,128)(2,1)S(1)} %broadcast_in_dim.55), channel_id=1, replica_groups=mesh['tp'=4,'rep_0'=4,'rep_1'=8,'rep_2'=2] {'rep_2'}, dimensions={0} | all-to-all | bytes 4194304 | tf_op jit(solution)/shard_map/all_to_all | solution.py:25
  55.4 0.8 fusion.14
  56.3 19.5 %all_to_all.46 = f32[4,1024,72]{1,2,0:T(8,128)S(1)} all-to-all(f32[4,1024,72]{1,2,0:T(8,128)S(1)} %broadcast_in_dim.56), channel_id=1, replica_groups=mesh['tp'=4,'rep_0'=4,'rep_1'=8,'rep_2'=2] {'tp'}, dimensions={0} | all-to-all | bytes 2359296 | tf_op jit(solution)/shard_map/all_to_all | solution.py:25
  75.8 0.8 reduce_sum.100
  76.6 1.0 multiply_reduce_fusion
  77.6 0.8 broadcast_in_dim.57
  78.4 7.1 %all-to-all-start.3 = ((f32[64,1,1024]{2,1,0:T(1,128)}), f32[64,1,1024]{2,1,0:T(1,128)S(1)}, u32[]{:S(2)}, u32[]{:S(2)}) async-start(f32[64,1,1024]{2,1,0:T(1,128)} %broadcast_in_dim.57), calls=%async_computation.3 | async-start | bytes 524288 | tf_op jit(solution)/shard_map/all_to_all | solution.py:25
  85.5 0.8 dynamic_slice.6
  86.3 11.2 %all-to-all-done.3 = f32[64,1,1024]{2,1,0:T(1,128)S(1)} async-done(((f32[64,1,1024]{2,1,0:T(1,128)}), f32[64,1,1024]{2,1,0:T(1,128)S(1)}, u32[]{:S(2)}, u32[]{:S(2)}) %all-to-all-start.3) | async-done | bytes 262176 | tf_op jit(solution)/shard_map/all_to_all | solution.py:25
  97.6 1.1 multiply_convert_fusion
  98.7 4.9 %stack.2 = bf16[64,1024,72]{1,2,0:T(8,128)(2,1)} broadcast(bf16[1024,72]{0,1:T(8,128)(2,1)S(1)} %multiply_convert_fusion), dimensions={1,2} | broadcast | bytes 9584640 | tf_op jit(solution)/shard_map/stack | solution.py:19
  103.6 6.3 %all-to-all-start.4 = ((bf16[64,1024,72]{1,2,0:T(8,128)(2,1)}), bf16[64,1024,72]{1,2,0:T(8,128)(2,1)}, u32[]{:S(2)}, u32[]{:S(2)}) async-start(bf16[64,1024,72]{1,2,0:T(8,128)(2,1)} %stack.2), calls=%async_computation.4 | async-start | bytes 18874368 | tf_op jit(solution)/shard_map/all_to_all | solution.py:19
  110.0 208.1 %all-to-all-done.4 = bf16[64,1024,72]{1,2,0:T(8,128)(2,1)} async-done(((bf16[64,1024,72]{1,2,0:T(8,128)(2,1)}), bf16[64,1024,72]{1,2,0:T(8,128)(2,1)}, u32[]{:S(2)}, u32[]{:S(2)}) %all-to-all-start.4) | async-done | bytes 9437216 | tf_op jit(solution)/shard_map/all_to_all | solution.py:19
  318.8 5.8 %all-to-all-start.7 = ((f32[64,1,128]{2,1,0:T(1,128)}), f32[64,1,128]{2,1,0:T(1,128)S(1)}, u32[]{:S(2)}, u32[]{:S(2)}) async-start(f32[64,1,128]{2,1,0:T(1,128)} %broadcast_in_dim.100), calls=%async_computation.7 | async-start | bytes 65536 | tf_op jit(solution)/shard_map/all_to_all | solution.py:25
  324.6 15.7 %exponential_reduce_fusion = (f32[1024]{0:T(1024)S(1)}, f32[1024]{0:T(1024)S(1)}) fusion(s32[1024]{0:T(1024)S(1)} %copy-done.4, s32[1000]{0:T(1024)S(1)} %iota_add_fusion, bf16[1024,4608]{0,1:T(8,128)(2,1)} %bitcast.4, bf16[1000,4608]{1,0:T(8,128)(2,1)} %param.23), kind=kOutput, calls=%fused_computation.1 | convolution fusion | flops 9443325952 | bytes 18669472 | tf_op jit(solution)/shard_map/dot_general | solution.py:136
  341.1 7.2 %all-to-all-start.5 = ((f32[16,1,2048]{2,1,0:T(1,128)}), f32[16,1,2048]{2,1,0:T(1,128)S(1)}, u32[]{:S(2)}, u32[]{:S(2)}) async-start(f32[16,1,2048]{2,1,0:T(1,128)} %broadcast_in_dim.59), calls=%async_computation.5 | async-start | bytes 262144 | tf_op jit(solution)/shard_map/all_to_all | solution.py:25
  348.5 8.7 %all-to-all-done.5 = f32[16,1,2048]{2,1,0:T(1,128)S(1)} async-done(((f32[16,1,2048]{2,1,0:T(1,128)}), f32[16,1,2048]{2,1,0:T(1,128)S(1)}, u32[]{:S(2)}, u32[]{:S(2)}) %all-to-all-start.5) | async-done | bytes 131104 | tf_op jit(solution)/shard_map/all_to_all | solution.py:25
  358.0 4.8 %all-to-all-start.6 = ((f32[16,1,2048]{2,1,0:T(1,128)}), f32[16,1,2048]{2,1,0:T(1,128)S(1)}, u32[]{:S(2)}, u32[]{:S(2)}) async-start(f32[16,1,2048]{2,1,0:T(1,128)} %broadcast_in_dim.60), calls=%async_computation.6 | async-start | bytes 262144 | tf_op jit(solution)/shard_map/all_to_all | solution.py:25
  363.4 6.3 %all-to-all-done.6 = f32[16,1,2048]{2,1,0:T(1,128)S(1)} async-done(((f32[16,1,2048]{2,1,0:T(1,128)}), f32[16,1,2048]{2,1,0:T(1,128)S(1)}, u32[]{:S(2)}, u32[]{:S(2)}) %all-to-all-start.6) | async-done | bytes 131104 | tf_op jit(solution)/shard_map/all_to_all | solution.py:25
  (43 shorter events, 6.8 us)
Async XLA Ops:
  0.6 1.7 copy-start
  45.2 10.2 %copy-start.2 = (bf16[1024,72]{0,1:T(8,128)(2,1)S(1)}, bf16[1024,72]{0,1:T(8,128)(2,1)}, u32[]{:S(2)}) copy-start(bf16[1024,72]{0,1:T(8,128)(2,1)} %param.20) | copy-start | bytes 442372
  55.4 21.2 %copy-start.1 = (bf16[1024,72]{0,1:T(8,128)(2,1)S(1)}, bf16[1024,72]{0,1:T(8,128)(2,1)}, u32[]{:S(2)}) copy-start(bf16[1024,72]{0,1:T(8,128)(2,1)} %param.21) | copy-start | bytes 442372
  78.4 19.0 %all-to-all-start.3 = ((f32[64,1,1024]{2,1,0:T(1,128)}), f32[64,1,1024]{2,1,0:T(1,128)S(1)}, u32[]{:S(2)}, u32[]{:S(2)}) async-start(f32[64,1,1024]{2,1,0:T(1,128)} %broadcast_in_dim.57), calls=%async_computation.3 | async-start | bytes 524288 | tf_op jit(solution)/shard_map/all_to_all | solution.py:25
  103.6 6.4 %copy-start.5 = (s32[16]{0:T(128)S(1)}, s32[16]{0:T(128)}, u32[]{:S(2)}) copy-start(s32[16]{0:T(128)} %param.27) | copy-start | bytes 196
  103.6 6.4 %copy-start.6 = (f32[16]{0:T(128)S(1)}, f32[16]{0:T(128)}, u32[]{:S(2)}) copy-start(f32[16]{0:T(128)} %param.26) | copy-start | bytes 196
  103.6 221.0 %copy-start.4 = (s32[1024]{0:T(1024)S(1)}, s32[1024]{0:T(1024)}, u32[]{:S(2)}) copy-start(s32[1024]{0:T(1024)} %param.24) | copy-start | bytes 12292
  103.6 214.6 %all-to-all-start.4 = ((bf16[64,1024,72]{1,2,0:T(8,128)(2,1)}), bf16[64,1024,72]{1,2,0:T(8,128)(2,1)}, u32[]{:S(2)}, u32[]{:S(2)}) async-start(bf16[64,1024,72]{1,2,0:T(8,128)(2,1)} %stack.2), calls=%async_computation.4 | async-start | bytes 18874368 | tf_op jit(solution)/shard_map/all_to_all | solution.py:19
  318.8 21.6 %all-to-all-start.7 = ((f32[64,1,128]{2,1,0:T(1,128)}), f32[64,1,128]{2,1,0:T(1,128)S(1)}, u32[]{:S(2)}, u32[]{:S(2)}) async-start(f32[64,1,128]{2,1,0:T(1,128)} %broadcast_in_dim.100), calls=%async_computation.7 | async-start | bytes 65536 | tf_op jit(solution)/shard_map/all_to_all | solution.py:25
  324.6 45.1 %copy-start.3 = (f32[16]{0:T(128)S(1)}, f32[16]{0:T(128)}, u32[]{:S(2)}) copy-start(f32[16]{0:T(128)} %param.25) | copy-start | bytes 196
  341.1 16.1 %all-to-all-start.5 = ((f32[16,1,2048]{2,1,0:T(1,128)}), f32[16,1,2048]{2,1,0:T(1,128)S(1)}, u32[]{:S(2)}, u32[]{:S(2)}) async-start(f32[16,1,2048]{2,1,0:T(1,128)} %broadcast_in_dim.59), calls=%async_computation.5 | async-start | bytes 262144 | tf_op jit(solution)/shard_map/all_to_all | solution.py:25
  358.0 11.6 %all-to-all-start.6 = ((f32[16,1,2048]{2,1,0:T(1,128)}), f32[16,1,2048]{2,1,0:T(1,128)S(1)}, u32[]{:S(2)}, u32[]{:S(2)}) async-start(f32[16,1,2048]{2,1,0:T(1,128)} %broadcast_in_dim.60), calls=%async_computation.6 | async-start | bytes 262144 | tf_op jit(solution)/shard_map/all_to_all | solution.py:25
